TPU v7x, 32 devices: a whole 2x2x4 slice. The times are simulated.
32 devices in a mesh: ens: 2 (over y), space: 4 (over z), chan: 2 (over x), sub: 2 (over core).
Axes of the slice: x: 2, y: 2, z: 4, core: 2. Of those that a mesh axis runs over, the one named last changes fastest.
Arguments:
- node_state: bfloat16 [8192, 512], P(('ens', 'space'), ('chan', 'sub')), parts along dimension 0, may hold values from -6 to 6
- norm_gains: float32 [2, 512], replicated, may hold values from 0.25 to 1.75
- norm_shifts: float32 [2, 512], replicated, may hold values from -3 to 3
- query_weight: bfloat16 [512, 512], P(None, 'chan')
- key_weight: bfloat16 [512, 512], P(None, 'chan')
- value_weight: bfloat16 [512, 512], P(None, 'chan'), may hold values from -0.25 to 0.25
- out_weight: bfloat16 [512, 512], replicated, may hold values from -0.25 to 0.25
- ffn_in: bfloat16 [2048, 512], P('chan'), may hold values from -0.25 to 0.25
- ffn_out: bfloat16 [2048, 512], P('chan'), may hold values from -0.125 to 0.125
- live_counts: int32 [4], P('space'), may hold values from 512 to 1024, as said below
- send_rows: int32 [4, 2, 256], P('space'), may hold values from 0 to 1023, as said below
- tile_keys: int32 [32, 12], P('space'), may hold values from 0 to 11, as said below
- tile_bits: int32 [32, 12, 4, 128], P('space'), may hold values from -2147483648 to 2147483647, as said below
Outputs:
- updated: bfloat16 [8192, 512], P(('ens', 'space'), ('chan', 'sub')), parts along dimension 0
There are 2 independent parts, one for each index of `ens`. A program takes and returns all parts, laid end to end along the dimension named above; an argument that names none is the same for every part. Nothing has to cross between parts.
Inputs may be any that keep to these rules, and one draw needn't show every extreme that they name: Partition s has live nodes 0 to live_counts[s] - 1; the first and the last partition are full. send_rows[s, 0] lists nodes of partition s read by its lower neighbour, send_rows[s, 1] those read by its upper neighbour; all are live nodes, and entries may repeat. `tile_keys`: slot 0 of every block names the block itself (its index within the partition); other slots name blocks of the same partition (below 8), of the lower halo (from 8) or of the upper halo (from 10); the first partition names no lower halo and the last no upper halo. `tile_bits`: bit j of word w in column r of a slot says whether query r of the block may attend key 32 w + j of the slot's block (bit 31 is the sign bit); in slot 0 every query's own bit is set. Slots whose words are all zero carry no edges.
All inputs are finite; a program needn't handle non-finite values.
Results may differ from a plain program's by a relative error of at most 0.0095.
Values may be sent and summed in bfloat16 or wider, within the bound.
A program may use at most 64 MiB of HBM per device.

v0:
```python
import math
import jax
import jax.numpy as jnp
from jax import lax
from jax.sharding import PartitionSpec as P

HD = 64
NORM_EPS = 1e-05
NEG_FILL = -1e30


def padded_2(array, sides, width):
    for axis, dim in sides:
        size, length = (lax.axis_size(axis), array.shape[dim])
        up = [(i, (i + 1) % size) for i in range(size - 1)]
        down = [(j, i) for i, j in up]
        last = lax.slice_in_dim(array, length - width, length, axis=dim)
        leading = lax.slice_in_dim(array, 0, width, axis=dim)
        before = lax.ppermute(last, axis, up)
        after = lax.ppermute(leading, axis, down)
        array = jnp.concatenate([before, array, after], axis=dim)
    return array


def normalize_rows(source, gain_row, shift_row):
    row_mean = jnp.mean(source, axis=-1, keepdims=True)
    spread = jnp.mean(source * source, axis=-1, keepdims=True) - row_mean * row_mean
    return (source - row_mean) * lax.rsqrt(spread + NORM_EPS) * gain_row + shift_row


def unpack_allowed(key_bits, key_ids, live_count, tile_size, blocks_own):
    shifts = jnp.arange(32, dtype=jnp.int32)
    expanded = jnp.right_shift(key_bits[..., None, :], shifts[:, None]) & 1
    lead_shape = key_bits.shape[:-2]
    expanded = expanded.reshape(lead_shape + (tile_size, tile_size))
    key_index = key_ids[..., None] * tile_size + jnp.arange(tile_size, dtype=jnp.int32)
    key_live = (key_ids[..., None] >= blocks_own) | (key_index < live_count)
    slot_count = key_ids.shape[-1]
    slot_first = jnp.arange(slot_count, dtype=jnp.int32)[:, None, None] == 0
    diagonal = (
        jnp.arange(tile_size, dtype=jnp.int32)[:, None]
        == jnp.arange(tile_size, dtype=jnp.int32)[None, :]
    )
    own_bit = slot_first & diagonal[None]
    return (expanded == 1) & (key_live[..., None] | own_bit)


def hidden_term(rows, in_piece, out_piece):
    hidden = jax.nn.gelu(
        lax.dot_general(
            rows, in_piece, (((1,), (1,)), ((), ())), preferred_element_type=jnp.float32
        )
    ).astype(jnp.bfloat16)
    return jnp.dot(hidden, out_piece, preferred_element_type=jnp.float32)


def on_device(
    node_state,
    norm_gains,
    norm_shifts,
    query_weight,
    key_weight,
    value_weight,
    out_weight,
    ffn_in,
    ffn_out,
    live_counts,
    send_rows,
    tile_keys,
    tile_bits,
):
    n_chan = lax.axis_size("chan")
    n_sub = lax.axis_size("sub")
    groups = n_chan * n_sub
    chan_at = lax.axis_index("chan")
    sub_at = lax.axis_index("sub")
    node_rank = chan_at * n_sub + sub_at
    node_count = node_state.shape[0]
    tile_size = tile_bits.shape[-1]
    word_count = tile_bits.shape[-2]
    slot_count = tile_keys.shape[1]
    blocks_own = tile_keys.shape[0]
    per_rank = node_count // groups
    head_cols = query_weight.shape[1]
    heads_here = head_cols // HD
    halo_rows = send_rows.shape[-1]
    live_count = live_counts[0]

    def own_half(source):
        step_rows = source.shape[0] // groups
        shaped = source.reshape((n_chan, n_sub, step_rows) + source.shape[1:])
        picked = lax.dynamic_index_in_dim(shaped, sub_at, 1, keepdims=False)
        return picked.reshape((n_chan * step_rows,) + source.shape[1:])

    node_rows = lax.all_to_all(node_state, ("chan", "sub"), split_axis=0, concat_axis=1, tiled=True)
    pair_weight = jnp.concatenate([key_weight, value_weight], axis=1)
    gathered = lax.all_gather(node_state, ("chan", "sub"), axis=1, tiled=True)
    normed = normalize_rows(gathered.astype(jnp.float32), norm_gains[0], norm_shifts[0]).astype(
        jnp.bfloat16
    )
    key_values = jnp.dot(normed, pair_weight, preferred_element_type=jnp.float32).astype(
        jnp.bfloat16
    )
    queries = jnp.dot(own_half(normed), query_weight, preferred_element_type=jnp.float32).astype(
        jnp.bfloat16
    )
    send_list = send_rows.reshape(2 * halo_rows)
    outgoing = jnp.take(key_values, send_list, axis=0)
    padded = padded_2(outgoing, (("space", 0),), halo_rows)
    extended = jnp.concatenate([key_values, padded[:halo_rows], padded[-halo_rows:]], axis=0)
    key_blocks = extended.reshape(-1, tile_size, 2 * head_cols)
    key_ids = own_half(tile_keys)
    key_bits = own_half(tile_bits)
    block_total = key_ids.shape[0]
    per_round = math.gcd(block_total, 4)
    rounds = block_total // per_round
    score_scale = 1.0 / math.sqrt(HD)

    def attend(inputs):
        q_part, id_part, bit_part = inputs
        chosen = key_blocks[id_part]
        keys_part = chosen[..., :head_cols].reshape(
            per_round, slot_count, tile_size, heads_here, HD
        )
        values_part = chosen[..., head_cols:].reshape(
            per_round, slot_count, tile_size, heads_here, HD
        )
        scores = (
            jnp.einsum("grhd,gtkhd->ghrtk", q_part, keys_part, preferred_element_type=jnp.float32)
            * score_scale
        )
        allowed = unpack_allowed(bit_part, id_part, live_count, tile_size, blocks_own)
        allowed = jnp.transpose(allowed, (0, 3, 1, 2))[:, None]
        masked = jnp.where(allowed, scores, NEG_FILL)
        row_max = jnp.max(masked, axis=(3, 4), keepdims=True)
        weights = jnp.where(allowed, jnp.exp(scores - row_max), 0.0)
        row_total = jnp.sum(weights, axis=(3, 4))
        mixed_heads = jnp.einsum(
            "ghrtk,gtkhd->grhd",
            weights.astype(jnp.bfloat16),
            values_part,
            preferred_element_type=jnp.float32,
        )
        mixed_heads = mixed_heads / jnp.transpose(row_total, (0, 2, 1))[..., None]
        return mixed_heads.astype(jnp.bfloat16).reshape(per_round * tile_size, head_cols)

    query_groups = queries.reshape(rounds, per_round, tile_size, heads_here, HD)
    attended = lax.map(
        attend,
        (
            query_groups,
            key_ids.reshape(rounds, per_round, slot_count),
            key_bits.reshape(rounds, per_round, slot_count, word_count, tile_size),
        ),
    )
    mixed_rows = jnp.dot(
        lax.all_to_all(
            attended.reshape(n_chan, per_rank, head_cols),
            "chan",
            split_axis=0,
            concat_axis=2,
            tiled=True,
        )[0],
        out_weight,
        preferred_element_type=jnp.float32,
    )
    after_attn = node_rows.astype(jnp.float32) + mixed_rows
    normed_two = normalize_rows(after_attn, norm_gains[1], norm_shifts[1]).astype(jnp.bfloat16)
    all_rows = lax.all_gather(normed_two, "chan", axis=0, tiled=True)
    update = lax.psum_scatter(
        hidden_term(all_rows, ffn_in, ffn_out).astype(jnp.bfloat16),
        "chan",
        scatter_dimension=0,
        tiled=True,
    ).astype(jnp.float32)
    position = node_rank * per_rank + jnp.arange(per_rank, dtype=jnp.int32)
    result = jnp.where((position < live_count)[:, None], after_attn + update, 0.0).astype(
        jnp.bfloat16
    )
    return lax.all_to_all(result, ("chan", "sub"), split_axis=1, concat_axis=0, tiled=True)


def solution(mesh):
    in_specs = (
        P(("ens", "space"), ("chan", "sub")),
        P(),
        P(),
        P(None, "chan"),
        P(None, "chan"),
        P(None, "chan"),
        P(),
        P("chan", None),
        P("chan", None),
        P("space"),
        P("space", None, None),
        P("space", None),
        P("space", None, None, None),
    )
    out_specs = P(("ens", "space"), ("chan", "sub"))
    return jax.shard_map(
        on_device, mesh=mesh, in_specs=in_specs, out_specs=out_specs, check_vma=False
    )
```

profile of v0, /device:TPU:0, one launch (start us, length us, event | category | flops | bytes accessed | tf_op | source)
XLA Modules:
  0.0 127.1 jit_solution(3869248447497856356)
XLA Ops:
  6.5 0.7 all-gather.2.cloned.1.call-update
  7.3 4.2 %all-to-all-start = ((bf16[4,256,128]{2,1,0:T(8,128)(2,1)}), bf16[4,256,128]{2,1,0:T(8,128)(2,1)}, u32[]{:S(2)}, u32[]{:S(2)}) async-start(bf16[4,256,128]{2,1,0:T(8,128)(2,1)} %bitcast.86), calls=%async_computation | async-start | bytes 524288 | tf_op jit(solution)/shard_map/all_to_all | solution.py:95
  14.4 0.9 constant_dynamic-slice_fusion.1
  15.6 1.2 fusion.10
  16.9 0.8 fusion.59
  17.7 0.8 fusion.60
  18.5 10.0 %all-gather.2.cloned.1.call-done = bf16[1024,512]{1,0:T(8,128)(2,1)} async-done(((bf16[1024,128]{1,0:T(8,128)(2,1)}), bf16[1024,512]{1,0:T(8,128)(2,1)}) %all-gather.2.cloned.1.call-update) | async-done | bytes 1048592 | tf_op jit(solution)/shard_map/all_gather | solution.py:97
  28.5 1.6 %convert_reduce_fusion = (f32[1024]{0:T(1024)S(1)}, f32[1024]{0:T(1024)S(1)}) fusion(bf16[1024,512]{1,0:T(8,128)(2,1)} %all-gather.2.cloned.1.call-done), kind=kLoop, calls=%fused_computation.17 | loop fusion | flops 2095104 | bytes 1056768 | tf_op jit(solution)/shard_map/reduce_sum | solution.py:26
  30.1 1.7 %fusion.14 = bf16[1024,512]{1,0:T(8,128)(2,1)S(1)} fusion(bf16[1024,512]{1,0:T(8,128)(2,1)} %all-gather.2.cloned.1.call-done, f32[512]{0:T(512)S(1)} %bitcast.103, f32[512]{0:T(512)S(1)} %bitcast.102, f32[1024]{0:T(1024)S(1)} %get-tuple-element.41, f32[1024]{0:T(1024)S(1)} %get-tuple-element.40), kind=kLoop, calls=%fused_computation.22 | loop fusion | flops 3145728 | bytes 2109440 | tf_op jit(solution)/shard_map/convert_element_type | solution.py:98
  31.8 1.0 copy-done.2
  32.8 0.7 convolution_convert_fusion
  33.5 2.0 %gather_fusion = bf16[512,512]{1,0:T(8,128)(2,1)S(1)} fusion(bf16[1024,512]{1,0:T(8,128)(2,1)S(1)} %convolution_convert_fusion, s32[1024]{0:T(1024)S(1)} %pad_clamp_fusion.1), kind=kCustom, calls=%fused_computation | custom fusion | bytes 1050624 | tf_op jit(solution)/shard_map/jit(_take)/gather | solution.py:108
  35.7 3.4 %collective-permute-start = (bf16[256,512]{1,0:T(8,128)(2,1)S(1)}, bf16[256,512]{1,0:T(8,128)(2,1)S(1)}, u32[]{:S(2)}, u32[]{:S(2)}) collective-permute-start(bf16[256,512]{1,0:T(8,128)(2,1)S(1)} %get-tuple-element.34), channel_id=1, source_target_pairs={{0,4},{4,8},{8,12},{1,5},{5,9},{9,13},{2,6},{6,10},{10,14},{3,7},{... | collective-permute-start | bytes 786440 | tf_op jit(solution)/shard_map/ppermute | solution.py:19
  39.1 1.3 %collective-permute-start.1 = (bf16[256,512]{1,0:T(8,128)(2,1)S(1)}, bf16[256,512]{1,0:T(8,128)(2,1)}, u32[]{:S(2)}, u32[]{:S(2)}) collective-permute-start(bf16[256,512]{1,0:T(8,128)(2,1)S(1)} %get-tuple-element.35), channel_id=1, source_target_pairs={{4,0},{8,4},{12,8},{5,1},{9,5},{13,9},{6,2},{10,6},{14,10},{7,3},{... | collective-permute-start | bytes 786440 | tf_op jit(solution)/shard_map/ppermute | solution.py:20
  40.4 1.1 constant_dynamic-slice_fusion
  41.8 1.1 reshape.235
  42.9 2.2 %collective-permute-done = bf16[256,512]{1,0:T(8,128)(2,1)S(1)} collective-permute-done((bf16[256,512]{1,0:T(8,128)(2,1)S(1)}, bf16[256,512]{1,0:T(8,128)(2,1)S(1)}, u32[]{:S(2)}, u32[]{:S(2)}) %collective-permute-start) | collective-permute-done | bytes 262176 | tf_op jit(solution)/shard_map/ppermute | solution.py:19
  45.7 3.5 %collective-permute-done.1 = bf16[256,512]{1,0:T(8,128)(2,1)} collective-permute-done((bf16[256,512]{1,0:T(8,128)(2,1)S(1)}, bf16[256,512]{1,0:T(8,128)(2,1)}, u32[]{:S(2)}, u32[]{:S(2)}) %collective-permute-start.1) | collective-permute-done | bytes 262176 | tf_op jit(solution)/shard_map/ppermute | solution.py:20
  49.3 1.5 %pad_maximum_fusion = bf16[1536,512]{1,0:T(8,128)(2,1)S(1)} fusion(bf16[256,512]{1,0:T(8,128)(2,1)} %collective-permute-done.1, bf16[256,512]{1,0:T(8,128)(2,1)} %copy-done.5, bf16[1024,512]{1,0:T(8,128)(2,1)} %copy-done.1), kind=kLoop, calls=%fused_computation.32 | loop fusion | flops 4718592 | bytes 3145728 | tf_op jit(solution)/shard_map/concatenate | solution.py:110
  50.8 5.0 %gather_fusion.1 = bf16[48,128,512]{2,1,0:T(8,128)(2,1)} fusion(bf16[12,128,512]{2,1,0:T(8,128)(2,1)S(1)} %bitcast.77, s32[1024]{0:T(1024)S(1)} %pad_clamp_fusion), kind=kCustom, calls=%fused_computation.1 | custom fusion | bytes 12583104 | tf_op jit(solution)/shard_map/while/body/eval_jaxpr/gather | solution.py:121
  55.7 8.6 %copy.29 = bf16[48,128,512]{1,2,0:T(8,128)(2,1)} copy(bf16[48,128,512]{2,1,0:T(8,128)(2,1)} %gather_fusion.1) | data formatting | bytes 12582912 | tf_op jit(solution)/shard_map/while/body/eval_jaxpr/gather | solution.py:121
  64.4 3.6 %fusion.57 = (bf16[4,12,128,256]{2,3,1,0:T(8,128)(2,1)S(1)}, bf16[4,12,128,256]{2,3,1,0:T(8,128)(2,1)S(1)}) fusion(bf16[4,12,128,512]{2,3,1,0:T(8,128)(2,1)} %bitcast.78), kind=kLoop, calls=%fused_computation.83 | loop fusion | bytes 12582912 | tf_op jit(solution)/shard_map/while/body/eval_jaxpr/slice | solution.py:125
  68.0 3.1 %select_reduce_fusion = (f32[4,4,128]{2,1,0:T(4,128)S(1)}, f32[4,4,128,12,128]{2,4,3,1,0:T(8,128)S(1)}) fusion(pred[4,128,12,128]{1,3,2,0:T(8,128)(4,1)S(1)} %bitcast.79, bf16[4,12,128,4,64]{2,4,3,1,0:T(8,128)(2,1)S(1)} %bitcast.83, bf16[4,128,4,64,1]{3,2,1,0,4:T(4,128)(2,1)S(1)} %bitcast.89), kind=kOutput, calls=%fused_computation.3 | convolution fusion | flops 412088320 | bytes 16785408 | tf_op jit(solution)/shard_map/while/body/eval_jaxpr/grhd,gtkhd->ghrtk/dot_general | solution.py:129
  71.1 2.8 %fusion = f32[4,4,128]{2,1,0:T(4,128)S(1)} fusion(f32[4,4,128,12,128]{2,4,3,1,0:T(8,128)S(1)} %get-tuple-element.45, f32[4,4,128]{2,1,0:T(4,128)S(1)} %get-tuple-element.44, pred[4,128,12,128]{1,3,2,0:T(8,128)(4,1)S(1)} %bitcast.80), kind=kLoop, calls=%fused_computation.4 | loop fusion | flops 12580864 | bytes 13385728 | tf_op jit(solution)/shard_map/while/body/eval_jaxpr/reduce_sum | solution.py:137
  73.9 3.4 %fusion.38 = bf16[4,128,4,64]{1,3,2,0:T(8,128)(2,1)S(1)} fusion(f32[4,4,128,12,128]{2,4,3,1,0:T(8,128)S(1)} %get-tuple-element.45, f32[4,4,128]{2,1,0:T(4,128)S(1)} %get-tuple-element.44, pred[4,128,12,128]{1,3,2,0:T(8,128)(4,1)S(1)} %bitcast.81, bf16[4,12,128,4,64]{2,4,3,1,0:T(8,128)(2,1)S(1)} %bitcast.82, f32[4,128,4]{1,2,0:T(4,128)S(1)} %bitcast.93), kind=kOutput, calls=%fused_computation.42 | convolution fusion | flops 415498240 | bytes 16793600 | tf_op jit(solution)/shard_map/while/body/eval_jaxpr/ghrtk,gtkhd->grhd/dot_general | solution.py:138
  77.8 7.6 %all_to_all.47 = bf16[2,256,256]{1,2,0:T(8,128)(2,1)S(1)} all-to-all(bf16[2,256,256]{1,2,0:T(8,128)(2,1)S(1)} %copy.36), channel_id=1, replica_groups=mesh['ens'=2,'space'=4,'chan'=2,'sub'=2] {'chan'}, dimensions={0} | all-to-all | bytes 524288 | tf_op jit(solution)/shard_map/all_to_all | solution.py:157
  85.4 1.4 %fusion.56 = (f32[256]{0:T(256)S(1)}, f32[256]{0:T(256)S(1)}, f32[256,512]{1,0:T(8,128)S(1)}) fusion(bf16[256,512]{0,1:T(8,128)(2,1)S(1)} %bitcast.88, bf16[512,512]{1,0:T(8,128)(2,1)S(1)} %copy-done.4, bf16[4,256,128]{2,1,0:T(8,128)(2,1)} %all-to-all-done), kind=kOutput, calls=%fused_computation.82 | convolution fusion | flops 134872576 | bytes 1574912 | tf_op jit(solution)/shard_map/dot_general | solution.py:156
  87.0 7.0 %all_gather.7 = bf16[512,512]{1,0:T(8,128)(2,1)S(1)} all-gather(bf16[256,512]{1,0:T(8,128)(2,1)S(1)} %add_convert_fusion), channel_id=1, replica_groups=mesh['ens'=2,'space'=4,'chan'=2,'sub'=2] {'chan'}, dimensions={0}, use_global_device_ids=true | all-gather | bytes 786432 | tf_op jit(solution)/shard_map/all_gather | solution.py:169
  94.0 2.3 %convolution_convert_fusion.1 = bf16[512,512]{1,0:T(8,128)(2,1)} fusion(bf16[1024,512]{1,0:T(8,128)(2,1)S(1)} %copy-done, bf16[512,512]{1,0:T(8,128)(2,1)S(1)} %all_gather.7, bf16[1024,512]{1,0:T(8,128)(2,1)S(1)} %copy-done.7), kind=kOutput, calls=%fused_computation.34 | convolution fusion | flops 1078722560 | bytes 3145728 | tf_op jit(solution)/shard_map/dot_general | solution.py:54
  96.3 13.8 %reduce-scatter.2.cloned.1.call-done = bf16[256,512]{1,0:T(8,128)(2,1)} async-done(((bf16[512,512]{1,0:T(8,128)(2,1)}), bf16[256,512]{1,0:T(8,128)(2,1)}) %reduce-scatter.2.cloned.1.call-update) | async-done | bytes 262160 | tf_op jit(solution)/shard_map/reduce_scatter | solution.py:170
  110.1 1.1 copy_bitcast_fusion
  111.2 8.4 %all_to_all.48 = bf16[256,4,128]{2,0,1:T(8,128)(2,1)S(1)} all-to-all(bf16[256,4,128]{2,0,1:T(8,128)(2,1)S(1)} %copy_bitcast_fusion), channel_id=1, replica_groups=mesh['ens'=2,'space'=4,'chan'=2,'sub'=2] {'chan','sub'}, dimensions={1} | all-to-all | bytes 524288 | tf_op jit(solution)/shard_map/all_to_all | solution.py:180
  (51 shorter events, 5.1 us)
Async XLA Ops:
  6.5 87.5 %copy-start = (bf16[1024,512]{1,0:T(8,128)(2,1)S(1)}, bf16[1024,512]{1,0:T(8,128)(2,1)}, u32[]{:S(2)}) copy-start(bf16[1024,512]{1,0:T(8,128)(2,1)} %param.21) | copy-start | bytes 3145732
  6.5 26.2 %copy-start.9 = (bf16[512,256]{1,0:T(8,128)(2,1)S(1)}, bf16[512,256]{1,0:T(8,128)(2,1)}, u32[]{:S(2)}) copy-start(bf16[512,256]{1,0:T(8,128)(2,1)} %param.17) | copy-start | bytes 786436
  6.5 26.2 %copy-start.8 = (bf16[512,256]{1,0:T(8,128)(2,1)S(1)}, bf16[512,256]{1,0:T(8,128)(2,1)}, u32[]{:S(2)}) copy-start(bf16[512,256]{1,0:T(8,128)(2,1)} %param.18) | copy-start | bytes 786436
  6.5 21.9 %all-gather.2.cloned.1.call-start = ((), (), s32[]{:S(2)}) async-start(), calls=%async_computation.4 | async-start | bytes 1310720 | tf_op jit(solution)/shard_map/all_gather | solution.py:97
  7.3 70.6 %all-to-all-start = ((bf16[4,256,128]{2,1,0:T(8,128)(2,1)}), bf16[4,256,128]{2,1,0:T(8,128)(2,1)}, u32[]{:S(2)}, u32[]{:S(2)}) async-start(bf16[4,256,128]{2,1,0:T(8,128)(2,1)} %bitcast.86), calls=%async_computation | async-start | bytes 524288 | tf_op jit(solution)/shard_map/all_to_all | solution.py:95
  11.5 98.6 %reduce-scatter.2.cloned.1.call-start = ((), (), s32[]{:S(2)}) async-start(), calls=%async_computation.5 | async-start | bytes 786432 | tf_op jit(solution)/shard_map/reduce_scatter | solution.py:170
  31.7 1.0 copy-start.2
  33.5 2.2 %copy-start.1 = (bf16[1024,512]{1,0:T(8,128)(2,1)}, bf16[1024,512]{1,0:T(8,128)(2,1)S(1)}, u32[]{:S(2)}) copy-start(bf16[1024,512]{1,0:T(8,128)(2,1)S(1)} %convolution_convert_fusion) | copy-start | bytes 3145732
  35.5 6.0 %copy-start.6 = (bf16[512,256]{1,0:T(8,128)(2,1)S(1)}, bf16[512,256]{1,0:T(8,128)(2,1)}, u32[]{:S(2)}) copy-start(bf16[512,256]{1,0:T(8,128)(2,1)} %param.16) | copy-start | bytes 786436
  35.7 9.3 %collective-permute-start = (bf16[256,512]{1,0:T(8,128)(2,1)S(1)}, bf16[256,512]{1,0:T(8,128)(2,1)S(1)}, u32[]{:S(2)}, u32[]{:S(2)}) collective-permute-start(bf16[256,512]{1,0:T(8,128)(2,1)S(1)} %get-tuple-element.34), channel_id=1, source_target_pairs={{0,4},{4,8},{8,12},{1,5},{5,9},{9,13},{2,6},{6,10},{10,14},{3,7},{... | collective-permute-start | bytes 786440 | tf_op jit(solution)/shard_map/ppermute | solution.py:19
  39.1 10.2 %collective-permute-start.1 = (bf16[256,512]{1,0:T(8,128)(2,1)S(1)}, bf16[256,512]{1,0:T(8,128)(2,1)}, u32[]{:S(2)}, u32[]{:S(2)}) collective-permute-start(bf16[256,512]{1,0:T(8,128)(2,1)S(1)} %get-tuple-element.35), channel_id=1, source_target_pairs={{4,0},{8,4},{12,8},{5,1},{9,5},{13,9},{6,2},{10,6},{14,10},{7,3},{... | collective-permute-start | bytes 786440 | tf_op jit(solution)/shard_map/ppermute | solution.py:20
  45.0 0.7 copy-start.5
  64.4 3.6 %copy-start.3 = (bf16[4,128,4,64]{3,2,1,0:T(4,128)(2,1)S(1)}, bf16[4,128,4,64]{3,2,1,0:T(4,128)(2,1)}, u32[]{:S(2)}) copy-start(bf16[4,128,4,64]{3,2,1,0:T(4,128)(2,1)} %reshape.235) | copy-start | bytes 786436
  73.9 11.5 %copy-start.4 = (bf16[512,512]{1,0:T(8,128)(2,1)S(1)}, bf16[512,512]{1,0:T(8,128)(2,1)}, u32[]{:S(2)}) copy-start(bf16[512,512]{1,0:T(8,128)(2,1)} %param.19) | copy-start | bytes 1572868
  77.4 16.6 %copy-start.7 = (bf16[1024,512]{1,0:T(8,128)(2,1)S(1)}, bf16[1024,512]{1,0:T(8,128)(2,1)}, u32[]{:S(2)}) copy-start(bf16[1024,512]{1,0:T(8,128)(2,1)} %param.20) | copy-start | bytes 3145732
Sparse Core Ops, SparseCore 0:
  8.9 19.5 all-gather.1
  96.4 13.6 reduce-scatter.1
where the time goes:
time: 128 us; the launch traced here: 127 us
  waiting for transfers between devices  30.2 us (24%)
  local copies, waits for them, and re-layouts  28.3 us (22%)
  blocking collectives  23 us (18%)
  between operations  14.3 us (11%)
  other arithmetic  11.2 us (9%)
  matrix products  11.2 us (9%)
  starting transfers between devices  8.95 us (7%)
    reduce_scatter x1, waiting for transfers between devices, on_device(): lax.psum_scatter(hidden_term(all_rows, ffn_in, ffn_out).astype(jnp.bfloat...  13.8 us
    gather x2, local copies, waits for them, and re-layouts, attend(): chosen = key_blocks[id_part]  13.6 us
    all_gather x1, waiting for transfers between devices, on_device(): gathered = lax.all_gather(node_state, ('chan', 'sub'), axis=1, tiled=True)  10 us
    all_to_all x1, blocking collectives, on_device(): lax.all_to_all(result, ('chan', 'sub'), split_axis=1, concat_axis=0, tile...  8.39 us
    all_to_all x1, blocking collectives, on_device(): lax.all_to_all(attended.reshape(n_chan, per_rank, head_cols), 'chan', spl...  7.56 us
    all_gather x1, blocking collectives, on_device(): all_rows = lax.all_gather(normed_two, 'chan', axis=0, tiled=True)  7.04 us
    all_to_all x1, starting transfers between devices, on_device(): lax.all_to_all(node_state, ('chan', 'sub'), split_axis=0, concat_axis=1,...  4.25 us
    unnamed x23, local copies, waits for them, and re-layouts  3.83 us
  transfers between devices with their start and end apart: 5, of which 4 were waited for; matrix products, arithmetic and copies ran while one was open for 34% of the time, Pallas kernels for 0%

commit v1 on v0

--- a/solution.py
+++ b/solution.py
@@ -177,7 +177,15 @@
     result = jnp.where((position < live_count)[:, None], after_attn + update, 0.0).astype(
         jnp.bfloat16
     )
-    return lax.all_to_all(result, ("chan", "sub"), split_axis=1, concat_axis=0, tiled=True)
+    return jnp.concatenate(
+        lax.all_to_all(
+            jnp.stack(jnp.split(result, lax.axis_size(("chan", "sub")), axis=1)),
+            ("chan", "sub"),
+            0,
+            0,
+        ),
+        axis=0,
+    )
 
 
 def solution(mesh):

time: 128 us -> 128 us (level)
  no operation moved by 1% of the time
where the time goes in v1:
time: 128 us; the launch traced here: 127 us
  waiting for transfers between devices  30.2 us (24%)
  local copies, waits for them, and re-layouts  28.3 us (22%)
  blocking collectives  23 us (18%)
  between operations  14.4 us (11%)
  other arithmetic  11.2 us (9%)
  matrix products  11.2 us (9%)
  starting transfers between devices  8.95 us (7%)
    reduce_scatter x1, waiting for transfers between devices, on_device(): lax.psum_scatter(hidden_term(all_rows, ffn_in, ffn_out).astype(jnp.bfloat...  13.8 us
    gather x2, local copies, waits for them, and re-layouts, attend(): chosen = key_blocks[id_part]  13.6 us
    all_gather x1, waiting for transfers between devices, on_device(): gathered = lax.all_gather(node_state, ('chan', 'sub'), axis=1, tiled=True)  10 us
    all_to_all x1, blocking collectives, on_device(): lax.all_to_all(jnp.stack(jnp.split(result, lax.axis_size(('chan', 'sub'))...  8.39 us
    all_to_all x1, blocking collectives, on_device(): lax.all_to_all(attended.reshape(n_chan, per_rank, head_cols), 'chan', spl...  7.56 us
    all_gather x1, blocking collectives, on_device(): all_rows = lax.all_gather(normed_two, 'chan', axis=0, tiled=True)  7.04 us
    all_to_all x1, starting transfers between devices, on_device(): lax.all_to_all(node_state, ('chan', 'sub'), split_axis=0, concat_axis=1,...  4.25 us
    unnamed x23, local copies, waits for them, and re-layouts  3.82 us
  transfers between devices with their start and end apart: 5, of which 4 were waited for; matrix products, arithmetic and copies ran while one was open for 34% of the time, Pallas kernels for 0%

profile of v1, /device:TPU:0, one launch (start us, length us, event | category | flops | bytes accessed | tf_op | source)
XLA Modules:
  0.0 127.2 jit_solution(5159760793971322)
XLA Ops:
  6.5 0.7 all-gather.2.cloned.1.call-update
  7.3 4.2 %all-to-all-start = ((bf16[4,256,128]{2,1,0:T(8,128)(2,1)}), bf16[4,256,128]{2,1,0:T(8,128)(2,1)}, u32[]{:S(2)}, u32[]{:S(2)}) async-start(bf16[4,256,128]{2,1,0:T(8,128)(2,1)} %bitcast.87), calls=%async_computation | async-start | bytes 524288 | tf_op jit(solution)/shard_map/all_to_all | solution.py:95
  14.4 0.9 constant_dynamic-slice_fusion.1
  15.6 1.2 fusion.10
  16.9 0.8 fusion.58
  17.7 0.8 fusion.59
  18.5 10.0 %all-gather.2.cloned.1.call-done = bf16[1024,512]{1,0:T(8,128)(2,1)} async-done(((bf16[1024,128]{1,0:T(8,128)(2,1)}), bf16[1024,512]{1,0:T(8,128)(2,1)}) %all-gather.2.cloned.1.call-update) | async-done | bytes 1048592 | tf_op jit(solution)/shard_map/all_gather | solution.py:97
  28.5 1.6 %convert_reduce_fusion = (f32[1024]{0:T(1024)S(1)}, f32[1024]{0:T(1024)S(1)}) fusion(bf16[1024,512]{1,0:T(8,128)(2,1)} %all-gather.2.cloned.1.call-done), kind=kLoop, calls=%fused_computation.17 | loop fusion | flops 2095104 | bytes 1056768 | tf_op jit(solution)/shard_map/reduce_sum | solution.py:26
  30.1 1.7 %fusion.14 = bf16[1024,512]{1,0:T(8,128)(2,1)S(1)} fusion(bf16[1024,512]{1,0:T(8,128)(2,1)} %all-gather.2.cloned.1.call-done, f32[512]{0:T(512)S(1)} %bitcast.104, f32[512]{0:T(512)S(1)} %bitcast.103, f32[1024]{0:T(1024)S(1)} %get-tuple-element.45, f32[1024]{0:T(1024)S(1)} %get-tuple-element.44), kind=kLoop, calls=%fused_computation.22 | loop fusion | flops 3145728 | bytes 2109440 | tf_op jit(solution)/shard_map/convert_element_type | solution.py:98
  31.8 1.0 copy-done.2
  32.8 0.7 convolution_convert_fusion
  33.5 2.0 %gather_fusion = bf16[512,512]{1,0:T(8,128)(2,1)S(1)} fusion(bf16[1024,512]{1,0:T(8,128)(2,1)S(1)} %convolution_convert_fusion, s32[1024]{0:T(1024)S(1)} %pad_clamp_fusion.1), kind=kCustom, calls=%fused_computation | custom fusion | bytes 1050624 | tf_op jit(solution)/shard_map/jit(_take)/gather | solution.py:108
  35.7 3.4 %collective-permute-start = (bf16[256,512]{1,0:T(8,128)(2,1)S(1)}, bf16[256,512]{1,0:T(8,128)(2,1)S(1)}, u32[]{:S(2)}, u32[]{:S(2)}) collective-permute-start(bf16[256,512]{1,0:T(8,128)(2,1)S(1)} %get-tuple-element.34), channel_id=1, source_target_pairs={{0,4},{4,8},{8,12},{1,5},{5,9},{9,13},{2,6},{6,10},{10,14},{3,7},{... | collective-permute-start | bytes 786440 | tf_op jit(solution)/shard_map/ppermute | solution.py:19
  39.1 1.3 %collective-permute-start.1 = (bf16[256,512]{1,0:T(8,128)(2,1)S(1)}, bf16[256,512]{1,0:T(8,128)(2,1)}, u32[]{:S(2)}, u32[]{:S(2)}) collective-permute-start(bf16[256,512]{1,0:T(8,128)(2,1)S(1)} %get-tuple-element.35), channel_id=1, source_target_pairs={{4,0},{8,4},{12,8},{5,1},{9,5},{13,9},{6,2},{10,6},{14,10},{7,3},{... | collective-permute-start | bytes 786440 | tf_op jit(solution)/shard_map/ppermute | solution.py:20
  40.4 1.1 constant_dynamic-slice_fusion
  41.8 1.1 reshape.236
  42.9 2.2 %collective-permute-done = bf16[256,512]{1,0:T(8,128)(2,1)S(1)} collective-permute-done((bf16[256,512]{1,0:T(8,128)(2,1)S(1)}, bf16[256,512]{1,0:T(8,128)(2,1)S(1)}, u32[]{:S(2)}, u32[]{:S(2)}) %collective-permute-start) | collective-permute-done | bytes 262176 | tf_op jit(solution)/shard_map/ppermute | solution.py:19
  45.7 3.5 %collective-permute-done.1 = bf16[256,512]{1,0:T(8,128)(2,1)} collective-permute-done((bf16[256,512]{1,0:T(8,128)(2,1)S(1)}, bf16[256,512]{1,0:T(8,128)(2,1)}, u32[]{:S(2)}, u32[]{:S(2)}) %collective-permute-start.1) | collective-permute-done | bytes 262176 | tf_op jit(solution)/shard_map/ppermute | solution.py:20
  49.3 1.5 %pad_maximum_fusion = bf16[1536,512]{1,0:T(8,128)(2,1)S(1)} fusion(bf16[256,512]{1,0:T(8,128)(2,1)} %collective-permute-done.1, bf16[256,512]{1,0:T(8,128)(2,1)} %copy-done.5, bf16[1024,512]{1,0:T(8,128)(2,1)} %copy-done.1), kind=kLoop, calls=%fused_computation.32 | loop fusion | flops 4718592 | bytes 3145728 | tf_op jit(solution)/shard_map/concatenate | solution.py:110
  50.8 5.0 %gather_fusion.1 = bf16[48,128,512]{2,1,0:T(8,128)(2,1)} fusion(bf16[12,128,512]{2,1,0:T(8,128)(2,1)S(1)} %bitcast.78, s32[1024]{0:T(1024)S(1)} %pad_clamp_fusion), kind=kCustom, calls=%fused_computation.1 | custom fusion | bytes 12583104 | tf_op jit(solution)/shard_map/while/body/eval_jaxpr/gather | solution.py:121
  55.7 8.6 %copy.27 = bf16[48,128,512]{1,2,0:T(8,128)(2,1)} copy(bf16[48,128,512]{2,1,0:T(8,128)(2,1)} %gather_fusion.1) | data formatting | bytes 12582912 | tf_op jit(solution)/shard_map/while/body/eval_jaxpr/gather | solution.py:121
  64.4 3.6 %fusion.56 = (bf16[4,12,128,256]{2,3,1,0:T(8,128)(2,1)S(1)}, bf16[4,12,128,256]{2,3,1,0:T(8,128)(2,1)S(1)}) fusion(bf16[4,12,128,512]{2,3,1,0:T(8,128)(2,1)} %bitcast.79), kind=kLoop, calls=%fused_computation.86 | loop fusion | bytes 12582912 | tf_op jit(solution)/shard_map/while/body/eval_jaxpr/slice | solution.py:125
  68.0 3.1 %select_reduce_fusion = (f32[4,4,128]{2,1,0:T(4,128)S(1)}, f32[4,4,128,12,128]{2,4,3,1,0:T(8,128)S(1)}) fusion(pred[4,128,12,128]{1,3,2,0:T(8,128)(4,1)S(1)} %bitcast.80, bf16[4,12,128,4,64]{2,4,3,1,0:T(8,128)(2,1)S(1)} %bitcast.84, bf16[4,128,4,64,1]{3,2,1,0,4:T(4,128)(2,1)S(1)} %bitcast.90), kind=kOutput, calls=%fused_computation.3 | convolution fusion | flops 412088320 | bytes 16785408 | tf_op jit(solution)/shard_map/while/body/eval_jaxpr/grhd,gtkhd->ghrtk/dot_general | solution.py:129
  71.1 2.8 %fusion = f32[4,4,128]{2,1,0:T(4,128)S(1)} fusion(f32[4,4,128,12,128]{2,4,3,1,0:T(8,128)S(1)} %get-tuple-element.49, f32[4,4,128]{2,1,0:T(4,128)S(1)} %get-tuple-element.48, pred[4,128,12,128]{1,3,2,0:T(8,128)(4,1)S(1)} %bitcast.81), kind=kLoop, calls=%fused_computation.4 | loop fusion | flops 12580864 | bytes 13385728 | tf_op jit(solution)/shard_map/while/body/eval_jaxpr/reduce_sum | solution.py:137
  74.0 3.4 %fusion.38 = bf16[4,128,4,64]{1,3,2,0:T(8,128)(2,1)S(1)} fusion(f32[4,4,128,12,128]{2,4,3,1,0:T(8,128)S(1)} %get-tuple-element.49, f32[4,4,128]{2,1,0:T(4,128)S(1)} %get-tuple-element.48, pred[4,128,12,128]{1,3,2,0:T(8,128)(4,1)S(1)} %bitcast.82, bf16[4,12,128,4,64]{2,4,3,1,0:T(8,128)(2,1)S(1)} %bitcast.83, f32[4,128,4]{1,2,0:T(4,128)S(1)} %bitcast.94), kind=kOutput, calls=%fused_computation.42 | convolution fusion | flops 415498240 | bytes 16793600 | tf_op jit(solution)/shard_map/while/body/eval_jaxpr/ghrtk,gtkhd->grhd/dot_general | solution.py:138
  77.8 7.6 %all_to_all.33 = bf16[2,256,256]{1,2,0:T(8,128)(2,1)S(1)} all-to-all(bf16[2,256,256]{1,2,0:T(8,128)(2,1)S(1)} %copy.34), channel_id=1, replica_groups=mesh['ens'=2,'space'=4,'chan'=2,'sub'=2] {'chan'}, dimensions={0} | all-to-all | bytes 524288 | tf_op jit(solution)/shard_map/all_to_all | solution.py:157
  85.4 1.4 %fusion.55 = (f32[256]{0:T(256)S(1)}, f32[256]{0:T(256)S(1)}, f32[256,512]{1,0:T(8,128)S(1)}) fusion(bf16[256,512]{0,1:T(8,128)(2,1)S(1)} %bitcast.89, bf16[512,512]{1,0:T(8,128)(2,1)S(1)} %copy-done.4, bf16[4,256,128]{2,1,0:T(8,128)(2,1)} %all-to-all-done), kind=kOutput, calls=%fused_computation.85 | convolution fusion | flops 134872576 | bytes 1574912 | tf_op jit(solution)/shard_map/dot_general | solution.py:156
  87.0 7.0 %all_gather.7 = bf16[512,512]{1,0:T(8,128)(2,1)S(1)} all-gather(bf16[256,512]{1,0:T(8,128)(2,1)S(1)} %add_convert_fusion), channel_id=1, replica_groups=mesh['ens'=2,'space'=4,'chan'=2,'sub'=2] {'chan'}, dimensions={0}, use_global_device_ids=true | all-gather | bytes 786432 | tf_op jit(solution)/shard_map/all_gather | solution.py:169
  94.0 2.3 %convolution_convert_fusion.1 = bf16[512,512]{1,0:T(8,128)(2,1)} fusion(bf16[1024,512]{1,0:T(8,128)(2,1)S(1)} %copy-done, bf16[512,512]{1,0:T(8,128)(2,1)S(1)} %all_gather.7, bf16[1024,512]{1,0:T(8,128)(2,1)S(1)} %copy-done.7), kind=kOutput, calls=%fused_computation.34 | convolution fusion | flops 1078722560 | bytes 3145728 | tf_op jit(solution)/shard_map/dot_general | solution.py:54
  96.3 13.8 %reduce-scatter.2.cloned.1.call-done = bf16[256,512]{1,0:T(8,128)(2,1)} async-done(((bf16[512,512]{1,0:T(8,128)(2,1)}), bf16[256,512]{1,0:T(8,128)(2,1)}) %reduce-scatter.2.cloned.1.call-update) | async-done | bytes 262160 | tf_op jit(solution)/shard_map/reduce_scatter | solution.py:170
  110.1 1.0 select_convert_fusion
  111.3 8.4 %all_to_all.34 = bf16[4,256,128]{2,1,0:T(8,128)(2,1)S(1)} all-to-all(bf16[4,256,128]{2,1,0:T(8,128)(2,1)S(1)} %pad_maximum_fusion.1), channel_id=1, replica_groups=mesh['ens'=2,'space'=4,'chan'=2,'sub'=2] {'chan','sub'}, dimensions={0} | all-to-all | bytes 524288 | tf_op jit(solution)/shard_map/all_to_all | solution.py:181
  (53 shorter events, 5.2 us)
Async XLA Ops:
  6.5 87.5 %copy-start = (bf16[1024,512]{1,0:T(8,128)(2,1)S(1)}, bf16[1024,512]{1,0:T(8,128)(2,1)}, u32[]{:S(2)}) copy-start(bf16[1024,512]{1,0:T(8,128)(2,1)} %param.21) | copy-start | bytes 3145732
  6.5 26.2 %copy-start.9 = (bf16[512,256]{1,0:T(8,128)(2,1)S(1)}, bf16[512,256]{1,0:T(8,128)(2,1)}, u32[]{:S(2)}) copy-start(bf16[512,256]{1,0:T(8,128)(2,1)} %param.17) | copy-start | bytes 786436
  6.5 26.2 %copy-start.8 = (bf16[512,256]{1,0:T(8,128)(2,1)S(1)}, bf16[512,256]{1,0:T(8,128)(2,1)}, u32[]{:S(2)}) copy-start(bf16[512,256]{1,0:T(8,128)(2,1)} %param.18) | copy-start | bytes 786436
  6.5 21.9 %all-gather.2.cloned.1.call-start = ((), (), s32[]{:S(2)}) async-start(), calls=%async_computation.4 | async-start | bytes 1310720 | tf_op jit(solution)/shard_map/all_gather | solution.py:97
  7.3 70.6 %all-to-all-start = ((bf16[4,256,128]{2,1,0:T(8,128)(2,1)}), bf16[4,256,128]{2,1,0:T(8,128)(2,1)}, u32[]{:S(2)}, u32[]{:S(2)}) async-start(bf16[4,256,128]{2,1,0:T(8,128)(2,1)} %bitcast.87), calls=%async_computation | async-start | bytes 524288 | tf_op jit(solution)/shard_map/all_to_all | solution.py:95
  11.5 98.6 %reduce-scatter.2.cloned.1.call-start = ((), (), s32[]{:S(2)}) async-start(), calls=%async_computation.5 | async-start | bytes 786432 | tf_op jit(solution)/shard_map/reduce_scatter | solution.py:170
  31.7 1.0 copy-start.2
  33.5 2.2 %copy-start.1 = (bf16[1024,512]{1,0:T(8,128)(2,1)}, bf16[1024,512]{1,0:T(8,128)(2,1)S(1)}, u32[]{:S(2)}) copy-start(bf16[1024,512]{1,0:T(8,128)(2,1)S(1)} %convolution_convert_fusion) | copy-start | bytes 3145732
  35.5 6.0 %copy-start.6 = (bf16[512,256]{1,0:T(8,128)(2,1)S(1)}, bf16[512,256]{1,0:T(8,128)(2,1)}, u32[]{:S(2)}) copy-start(bf16[512,256]{1,0:T(8,128)(2,1)} %param.16) | copy-start | bytes 786436
  35.7 9.3 %collective-permute-start = (bf16[256,512]{1,0:T(8,128)(2,1)S(1)}, bf16[256,512]{1,0:T(8,128)(2,1)S(1)}, u32[]{:S(2)}, u32[]{:S(2)}) collective-permute-start(bf16[256,512]{1,0:T(8,128)(2,1)S(1)} %get-tuple-element.34), channel_id=1, source_target_pairs={{0,4},{4,8},{8,12},{1,5},{5,9},{9,13},{2,6},{6,10},{10,14},{3,7},{... | collective-permute-start | bytes 786440 | tf_op jit(solution)/shard_map/ppermute | solution.py:19
  39.1 10.2 %collective-permute-start.1 = (bf16[256,512]{1,0:T(8,128)(2,1)S(1)}, bf16[256,512]{1,0:T(8,128)(2,1)}, u32[]{:S(2)}, u32[]{:S(2)}) collective-permute-start(bf16[256,512]{1,0:T(8,128)(2,1)S(1)} %get-tuple-element.35), channel_id=1, source_target_pairs={{4,0},{8,4},{12,8},{5,1},{9,5},{13,9},{6,2},{10,6},{14,10},{7,3},{... | collective-permute-start | bytes 786440 | tf_op jit(solution)/shard_map/ppermute | solution.py:20
  45.0 0.7 copy-start.5
  64.4 3.6 %copy-start.3 = (bf16[4,128,4,64]{3,2,1,0:T(4,128)(2,1)S(1)}, bf16[4,128,4,64]{3,2,1,0:T(4,128)(2,1)}, u32[]{:S(2)}) copy-start(bf16[4,128,4,64]{3,2,1,0:T(4,128)(2,1)} %reshape.236) | copy-start | bytes 786436
  73.9 11.5 %copy-start.4 = (bf16[512,512]{1,0:T(8,128)(2,1)S(1)}, bf16[512,512]{1,0:T(8,128)(2,1)}, u32[]{:S(2)}) copy-start(bf16[512,512]{1,0:T(8,128)(2,1)} %param.19) | copy-start | bytes 1572868
  77.4 16.6 %copy-start.7 = (bf16[1024,512]{1,0:T(8,128)(2,1)S(1)}, bf16[1024,512]{1,0:T(8,128)(2,1)}, u32[]{:S(2)}) copy-start(bf16[1024,512]{1,0:T(8,128)(2,1)} %param.20) | copy-start | bytes 3145732
Sparse Core Ops, SparseCore 0:
  8.9 19.5 all-gather.1
  96.4 13.6 reduce-scatter.1
